TPU v7x, 32 devices: a whole 2x2x4 slice. The times are simulated.
32 devices in a mesh: slab: 16 (over z, y, x), blk: 2 (over core).
Axes of the slice: x: 2, y: 2, z: 4, core: 2. Of those that a mesh axis runs over, the one named last changes fastest.
Arguments:
- slip_rate: float32 [32768], P('slab'), may hold values from 0.1 to 3
- log_state: float32 [32768], P('slab'), may hold values from -1 to 1
- friction_a: float32 [32768], P('slab'), may hold values from 0.2 to 1
- friction_b: float32 [32768], P('slab'), may hold values from 0.2 to 1
- normal_stress: float32 [32768], P('slab'), may hold values from 2 to 4
- leak_rate: float32 [32768], P('slab'), may hold values from 0.5 to 2
- corner: int32 [3, 32768], P(None, 'slab'), may hold values from 0 to 1022, as said below
- fraction: float32 [3, 32768], P(None, 'slab'), may hold values from 0 to 1
- near_blocks: bfloat16 [64, 3, 512, 512], P(('slab', 'blk')), may hold values from -0.15625 to 0.15625
- row_basis: bfloat16 [24, 32768], P(None, 'slab'), may hold values from -1.25 to 1.25
- col_basis: bfloat16 [24, 32768], P(None, 'slab'), may hold values from -0.25 to 0.25
- far_row: int32 [32768], P(('slab', 'blk')), may hold values from 0 to 3
- far_col: int32 [32768], P(('slab', 'blk')), may hold values from 0 to 63, as said below
- far_rank: int32 [32768], P(('slab', 'blk')), may hold values from 0 to 24, as said below
- far_coupling: bfloat16 [24, 24, 32768], P(None, None, ('slab', 'blk')), may hold values from -0.078125 to 0.078125
- pressure: float32 [32, 512, 1024], P('slab', 'blk'), may hold values from -1 to 1
- region: int32 [32, 512, 1024], P('slab', 'blk'), may hold values from 0 to 15
- perm_table: float32 [16], replicated, may hold values from 0.05 to 1
Outputs:
- slip_accel: float32 [32768], P('slab')
- state_rate: float32 [32768], P('slab')
- pressure_rate: float32 [32, 512, 1024], P('slab', 'blk')
Inputs may be any that keep to these rules, and one draw needn't show every extreme that they name: corner[0, f] equals 2 * (f // 2048), the first plane of the slab that holds cell f; corner[1, f] is at most 510 and corner[2, f] at most 1022. far_col[s] differs by 2 or more (cyclically over 64 clusters) from the slot's row cluster 4 * (s // 2048) + far_row[s]. `far_rank`: slots with rank 0 are empty; the live slots of a device come first, and some device has all 1024 slots live.
All inputs are finite; a program needn't handle non-finite values.
Results may differ from a plain program's by a relative error of at most 0.0022.
Values may be sent and summed in bfloat16 or wider, within the bound.
No kernel may reach another device: no remote copies, remote signals or barrier semaphores. Data moves between devices by JAX's collectives and lax.ppermute only.
A program may use at most 64 MiB of HBM per device.

v0:
```python
import functools

import jax
import jax.numpy as jnp
from jax import lax
from jax.experimental import pallas as pl
from jax.experimental.pallas import tpu as pltpu
from jax.sharding import PartitionSpec as P

VMEM = pltpu.MemorySpace.VMEM
SMEM = pltpu.MemorySpace.SMEM
SPLIT = (8,)


def row_chunks(rows):
    sizes = [rows * part // sum(SPLIT) for part in SPLIT]
    starts = [sum(sizes[:i]) for i in range(len(sizes))]
    return list(zip(starts, sizes))


def lookup(table, index):
    height, width = index.shape
    table = jnp.concatenate([table] * (height // 8), axis=0)
    parts = [
        jnp.take_along_axis(table, index[:, at : at + 128], axis=1) for at in range(0, width, 128)
    ]
    return jnp.concatenate(parts, axis=1)


def prepare_kernel(
    chunks, clusters, core_ref, p_ref, region_ref, p_edge_ref, region_edge_ref, slip_ref, basis_ref, *outs
):
    edge_ref, message_ref = outs[-2:]
    f32, bf16 = jnp.float32, jnp.bfloat16
    planes = p_edge_ref.shape[0]
    for (start, size), out in zip(chunks, outs):
        rows = pl.ds(start, size)
        out[0] = p_ref[0, rows, :].astype(bf16)
        out[1] = region_ref[0, rows, :].astype(f32).astype(bf16)
    low = core_ref[0] != 0
    for plane in range(planes):
        block, kind = p_edge_ref[plane], region_edge_ref[plane].astype(f32)
        edge_ref[plane : plane + 1, :] = jnp.where(low, block[0:1, :], block[7:8, :])
        edge_ref[planes + plane : planes + plane + 1, :] = jnp.where(low, kind[0:1, :], kind[7:8, :])
    cells = slip_ref.shape[1]
    size = cells // clusters
    per = size // 128
    slip = slip_ref[...].astype(bf16).astype(f32)
    lines = [slip[:, at : at + 128] for at in range(0, size, 128)]
    lines += [slip[:, at : at + 128] for at in range(cells - size, cells, 128)]
    rank = basis_ref.shape[0]
    for cluster in range(clusters):
        part = slip[:, cluster * size : (cluster + 1) * size].astype(bf16)
        moment = lax.dot_general(
            jnp.broadcast_to(part, (16, size)),
            basis_ref[:, cluster * size : (cluster + 1) * size],
            (((1,), (1,)), ((), ())),
            preferred_element_type=f32,
        )[0:1, :]
        lines.append(jnp.concatenate([moment, jnp.zeros((1, 128 - rank), f32)], axis=1))
    height = message_ref.shape[1]
    lines.append(jnp.zeros((height - len(lines), 128), f32))
    message = jnp.concatenate(lines, axis=0).astype(bf16)
    for slab in range(message_ref.shape[0]):
        message_ref[slab] = message


def prepare(pressure, region, slip, basis, core, chunks, clusters, slabs):
    planes, rows, width = pressure.shape
    cells = slip.shape[1]
    lines = 2 * (cells // clusters // 128) + clusters
    height = -(-lines // 16) * 16
    plane = pl.BlockSpec((1, rows, width), lambda i, core: (planes - 1, 0, 0))
    edge = pl.BlockSpec((planes, 8, width), lambda i, core: (0, (1 - core[0]) * (rows // 8 - 1), 0))
    full = lambda shape: pl.BlockSpec(shape, lambda i, core: (0,) * len(shape))
    shapes = [((2, size, width), jnp.bfloat16) for _, size in chunks]
    shapes += [((2 * planes, width), jnp.float32), ((slabs, height, 128), jnp.bfloat16)]
    return pl.pallas_call(
        functools.partial(prepare_kernel, chunks, clusters),
        grid_spec=pltpu.PrefetchScalarGridSpec(
            num_scalar_prefetch=1,
            grid=(1,),
            in_specs=[plane, plane, edge, edge, full(slip.shape), full(basis.shape)],
            out_specs=[full(shape) for shape, _ in shapes],
        ),
        out_shape=[jax.ShapeDtypeStruct(*shape) for shape in shapes],
        name="prepare",
    )(core, pressure, region, pressure, region, slip, basis)


def cells_kernel(start_ref, p_ref, corner_ref, fraction_ref, slip_ref, leak_ref, sampled_ref, source_ref, field):
    planes, rows, width = p_ref.shape
    cells = corner_ref.shape[1]
    step = pl.program_id(0)
    f32, bf16 = jnp.float32, jnp.bfloat16

    @pl.when(step == 0)
    def _():
        field[...] = p_ref[...].astype(bf16)

    frac = fraction_ref[...]
    at_y = corner_ref[1:2, :] - start_ref[0]
    at_z = corner_ref[2:3, :]
    high_z = frac[2:3, :]
    low_z = 1.0 - high_z
    low_hi, high_hi = low_z.astype(bf16).astype(f32), high_z.astype(bf16).astype(f32)
    iota = lax.broadcasted_iota(jnp.int32, (width, cells), 0)
    here, above = iota == at_z, iota == at_z + 1
    zero = jnp.float32(0.0)
    z_hi = jnp.where(here, low_hi, jnp.where(above, high_hi, zero)).astype(bf16)
    z_lo = jnp.where(here, low_z - low_hi, jnp.where(above, high_z - high_hi, zero)).astype(bf16)
    iota_y = lax.broadcasted_iota(jnp.int32, (rows, cells), 0)
    weight_y = jnp.where(
        iota_y == at_y, 1.0 - frac[1:2, :], jnp.where(iota_y == at_y + 1, frac[1:2, :], zero)
    )
    flow = slip_ref[...] * leak_ref[...]
    total = jnp.zeros((1, cells), f32)
    for plane in range(2):
        weight_x = frac[0:1, :] if plane else 1.0 - frac[0:1, :]
        along = jnp.dot(field[plane], z_hi, preferred_element_type=f32)
        total = total + weight_x * jnp.sum(weight_y * along, axis=0, keepdims=True)
        scaled = (weight_y * (weight_x * flow)).astype(bf16)
        dims = (((1,), (1,)), ((), ()))
        spread = lax.dot_general(scaled, z_hi, dims, preferred_element_type=f32)
        spread = spread + lax.dot_general(scaled, z_lo, dims, preferred_element_type=f32)

        @pl.when(step == 0)
        def _():
            source_ref[plane] = spread

        @pl.when(step != 0)
        def _():
            source_ref[plane] = source_ref[plane] + spread

    sampled_ref[...] = total


def cells(pressure, corner, fraction, slip, leak, y_start, block):
    planes, rows, width = pressure.shape
    count = corner.shape[1]
    vec = lambda n: pl.BlockSpec((n, block), lambda i: (0, i))
    whole = pl.BlockSpec((planes, rows, width), lambda i: (0, 0, 0))
    return pl.pallas_call(
        cells_kernel,
        grid=(count // block,),
        in_specs=[pl.BlockSpec(memory_space=SMEM), whole, vec(3), vec(3), vec(1), vec(1)],
        out_specs=[vec(1), whole],
        out_shape=[
            jax.ShapeDtypeStruct((1, count), jnp.float32),
            jax.ShapeDtypeStruct(pressure.shape, jnp.float32),
        ],
        scratch_shapes=[pltpu.VMEM(pressure.shape, jnp.bfloat16)],
        cost_estimate=pl.CostEstimate(
            flops=6 * planes * rows * width * count, bytes_accessed=4 * pressure.size * 2, transcendentals=0
        ),
        name="cells",
    )(y_start, pressure, corner, fraction, slip, leak)


def stencil_kernel(
    core_ref, table_ref, p_ref, p_before, p_after, k_ref, k_before, k_after, edge_ref, source_ref, low_ref,
    out_ref, pad_p, pad_r,
):
    planes, rows, width = p_ref.shape
    f32 = jnp.float32
    far = jnp.float32(jnp.inf)
    strips = rows // 16
    core = core_ref[0]
    step, last = pl.program_id(0), pl.num_programs(0) - 1
    table = table_ref[...]
    outside = jnp.full((8, width), far, f32)
    for plane in range(planes):
        pad_p[plane, 0:8, :] = p_before[plane]
        pad_r[plane, 0:8, :] = lookup(table, k_before[plane])
        pad_p[plane, rows + 8 : rows + 16, :] = p_after[plane]
        pad_r[plane, rows + 8 : rows + 16, :] = lookup(table, k_after[plane])

    for at_step, at, mine in ((0, 0, core != 0), (last, rows + 8, core == 0)):

        @pl.when(step == at_step)
        def _():
            for plane in range(planes):
                edge_p = jnp.broadcast_to(edge_ref[plane : plane + 1, :], (8, width))
                edge_k = edge_ref[planes + plane : planes + plane + 1, :].astype(jnp.int32)
                edge_r = lookup(table, jnp.broadcast_to(edge_k, (8, width)))
                pad_p[plane, at : at + 8, :] = edge_p
                pad_r[plane, at : at + 8, :] = jnp.where(mine, edge_r, outside)

    def fill(s, carry):
        at = pl.multiple_of(s * 8, 8)
        to = pl.multiple_of(s * 8 + 8, 8)
        for plane in range(planes):
            pad_p[plane, pl.ds(to, 8), :] = p_ref[plane, pl.ds(at, 8), :]
            pad_r[plane, pl.ds(to, 8), :] = lookup(table, k_ref[plane, pl.ds(at, 8), :])
        return carry

    lax.fori_loop(0, rows // 8, fill, 0)
    lane = lax.broadcasted_iota(jnp.int32, (8, width), 1)
    sub = lax.broadcasted_iota(jnp.int32, (8, width), 0)

    def face(p, r, p_next, r_next):
        return 2.0 / (r + r_next) * (p_next - p)

    def y_face(plane, at):
        p, r = pad_p[plane, pl.ds(at, 8), :], pad_r[plane, pl.ds(at, 8), :]
        after = pl.multiple_of(at + 8, 8)
        pn, rn = pad_p[plane, pl.ds(after, 8), :], pad_r[plane, pl.ds(after, 8), :]
        pn = pltpu.roll(jnp.where(sub == 0, pn, p), 7, 0)
        rn = pltpu.roll(jnp.where(sub == 0, rn, r), 7, 0)
        return p, r, face(p, r, pn, rn)

    def strip(to, low, carry):
        at = pl.multiple_of(to + 8, 8)
        after = []
        sums, ps, rs = [], [], []
        for plane in range(planes):
            p, r, fy = y_face(plane, at)
            below = pltpu.roll(jnp.where(sub == 7, carry[plane], fy), 1, 0)
            after.append(fy)
            pz = pltpu.roll(p, width - 1, 1)
            rz = jnp.where(lane == width - 1, far, pltpu.roll(r, width - 1, 1))
            fz = face(p, r, pz, rz)
            sums.append(fy - below + (fz - pltpu.roll(fz, 1, 1)))
            ps.append(p)
            rs.append(r)
        for plane in range(planes - 1):
            fx = face(ps[plane], rs[plane], ps[plane + 1], rs[plane + 1])
            sums[plane] = sums[plane] + fx
            sums[plane + 1] = sums[plane + 1] - fx
        sums[0] = sums[0] + low
        for plane in range(planes):
            out_ref[plane, pl.ds(to, 8), :] = source_ref[plane, pl.ds(to, 8), :] + sums[plane]
        return tuple(after)

    def body(s, carry):
        to = pl.multiple_of(s * 16, 16)
        low = low_ref[pl.ds(to, 16), :].astype(f32)
        carry = strip(to, low[:8], carry)
        return strip(pl.multiple_of(to + 8, 8), low[8:], carry)

    first = tuple(y_face(plane, 0)[2] for plane in range(planes))
    lax.fori_loop(0, strips, body, first)


def local_stencil(pressure, region, edge, source, low, table, core, block):
    planes, rows, width = pressure.shape
    smem = pl.BlockSpec(memory_space=SMEM)
    part = pl.BlockSpec((planes, block, width), lambda i: (0, i, 0))
    eighth = block // 8
    before = pl.BlockSpec((planes, 8, width), lambda i: (0, jnp.maximum(i * eighth - 1, 0), 0))
    after = pl.BlockSpec(
        (planes, 8, width), lambda i: (0, jnp.minimum((i + 1) * eighth, rows // 8 - 1), 0)
    )
    full = lambda shape: pl.BlockSpec(shape, lambda i: (0,) * len(shape))
    return pl.pallas_call(
        stencil_kernel,
        grid=(rows // block,),
        in_specs=[
            smem, full(table.shape), part, before, after, part, before, after, full(edge.shape), part,
            pl.BlockSpec((block, width), lambda i: (i, 0)),
        ],
        out_specs=part,
        out_shape=jax.ShapeDtypeStruct(pressure.shape, jnp.float32),
        scratch_shapes=[pltpu.VMEM((planes, block + 16, width), jnp.float32)] * 2,
        input_output_aliases={9: 0},
        cost_estimate=pl.CostEstimate(
            flops=200 * pressure.size, bytes_accessed=16 * pressure.size, transcendentals=0
        ),
        name="stencil",
    )(core, table, pressure, pressure, pressure, region, region, region, edge, source, low)


def face_kernel(valid_ref, table_ref, halo_ref, p_ref, region_ref, out_ref):
    valid = valid_ref[0] != 0
    far = jnp.float32(jnp.inf)
    table = table_ref[...]

    def body(s, carry):
        at = pl.multiple_of(s * 16, 16)
        rows = pl.ds(at, 16)
        other_p = halo_ref[0, rows, :].astype(jnp.float32)
        other_r = lookup(table, halo_ref[1, rows, :].astype(jnp.float32).astype(jnp.int32))
        other_r = jnp.where(valid, other_r, far)
        r = lookup(table, region_ref[0, rows, :])
        flux = 2.0 / (r + other_r) * (other_p - p_ref[0, rows, :])
        out_ref[rows, :] = flux.astype(jnp.bfloat16)
        return carry

    lax.fori_loop(0, out_ref.shape[0] // 16, body, 0)


def face_flux(halo, pressure, region, table, valid, start, block):
    size, width = halo.shape[1:]
    smem = pl.BlockSpec(memory_space=SMEM)
    rows = pl.BlockSpec((1, block, width), lambda i: (0, start // block + i, 0))
    return pl.pallas_call(
        face_kernel,
        grid=(size // block,),
        in_specs=[
            smem,
            pl.BlockSpec(table.shape, lambda i: (0, 0)),
            pl.BlockSpec((2, block, width), lambda i: (0, i, 0)),
            rows,
            rows,
        ],
        out_specs=pl.BlockSpec((block, width), lambda i: (i, 0)),
        out_shape=jax.ShapeDtypeStruct((size, width), jnp.bfloat16),
        name="face",
    )(valid, table, halo, pressure, region)


def finish_kernel(sign, flux_ref, acc_ref, out_ref):
    out_ref[0] = acc_ref[0] + sign * flux_ref[...].astype(jnp.float32)


def finish(acc, flux, plane, start, sign, block):
    planes, rows, width = acc.shape
    size = flux.shape[0]
    part = pl.BlockSpec((1, block, width), lambda i: (plane, start // block + i, 0))
    return pl.pallas_call(
        functools.partial(finish_kernel, sign),
        grid=(size // block,),
        in_specs=[pl.BlockSpec((block, width), lambda i: (i, 0)), part],
        out_specs=part,
        out_shape=jax.ShapeDtypeStruct(acc.shape, jnp.float32),
        input_output_aliases={1: 0},
        name="finish",
    )(flux, acc)


def traction_kernel(
    place_ref, got_ref, slip_ref, near_ref, coupling_ref, far_ref, basis_ref, out_ref, *, half_rows
):
    f32, bf16 = jnp.float32, jnp.bfloat16
    core, slab = place_ref[0], place_ref[1]
    slabs = got_ref.shape[0]
    rank, cells = basis_ref.shape
    size = near_ref.shape[2]
    clusters = cells // size
    per = size // 128
    slots = far_ref.shape[1]

    cols, rows, ranks = far_ref[0:1, :], far_ref[1:2, :], far_ref[2:3, :]
    owner, member = cols // clusters, cols % clusters
    slab_iota = lax.broadcasted_iota(jnp.int32, (slabs, slots), 0)
    pick = (slab_iota == owner).astype(f32).astype(bf16)
    picked = jnp.zeros((128, slots), f32)
    for cluster in range(clusters):
        sent = got_ref[:, 2 * per + cluster, :]
        chosen = lax.dot_general(sent, pick, (((0,), (0,)), ((), ())), preferred_element_type=f32)
        picked = jnp.where(member == cluster, chosen, picked)
    rank_iota = lax.broadcasted_iota(jnp.int32, (rank, slots), 0)
    masked = jnp.where(rank_iota < ranks, picked[:rank, :], jnp.float32(0.0))
    lines = []
    for a in range(rank):
        lines.append(jnp.sum(coupling_ref[a].astype(f32) * masked, axis=0, keepdims=True))
    block = jnp.concatenate(lines, axis=0)
    far = []
    for cluster in range(clusters):
        total = jnp.sum(jnp.where(rows == cluster, block, jnp.float32(0.0)), axis=1, keepdims=True)
        basis = basis_ref[:, cluster * size : (cluster + 1) * size].astype(f32)
        far.append(jnp.sum(basis * total, axis=0, keepdims=True))

    def line(slab_at, row):
        parts = [got_ref[pl.ds(slab_at, 1), row + i, :].astype(f32) for i in range(per)]
        return jnp.concatenate(parts, axis=1)

    zero = jnp.zeros((1, size), f32)
    before = jnp.where(slab > 0, line(jnp.maximum(slab - 1, 0), per), zero)
    after = jnp.where(slab < slabs - 1, line(jnp.minimum(slab + 1, slabs - 1), 0), zero)
    slip = slip_ref[...].astype(bf16).astype(f32)
    extended = [before] + [slip[:, c * size : (c + 1) * size] for c in range(clusters)] + [after]
    near = []
    for i in range(half_rows):
        total = jnp.zeros((16, size), f32)
        for j in range(3):
            source = jnp.where(core == 0, extended[i + j], extended[half_rows + i + j])
            total = total + lax.dot_general(
                jnp.broadcast_to(source, (16, size)).astype(bf16),
                near_ref[i, j],
                (((1,), (1,)), ((), ())),
                preferred_element_type=f32,
            )
        near.append(total[0:1, :])
    for cluster in range(clusters):
        mine = (cluster // half_rows) == core
        out_ref[:, cluster * size : (cluster + 1) * size] = far[cluster] + jnp.where(
            mine, near[cluster % half_rows], zero
        )


def traction_share(got, slip, near_blocks, far_coupling, far, row_basis, place):
    vmem, smem = pl.BlockSpec(memory_space=VMEM), pl.BlockSpec(memory_space=SMEM)
    return pl.pallas_call(
        functools.partial(traction_kernel, half_rows=near_blocks.shape[0]),
        in_specs=[smem] + [vmem] * 6,
        out_specs=vmem,
        out_shape=jax.ShapeDtypeStruct(slip.shape, jnp.float32),
        name="traction",
    )(place, got, slip, near_blocks, far_coupling, far, row_basis)


def shards(
    slip_rate,
    log_state,
    friction_a,
    friction_b,
    normal_stress,
    leak_rate,
    corner,
    fraction,
    near_blocks,
    row_basis,
    col_basis,
    far_row,
    far_col,
    far_rank,
    far_coupling,
    pressure,
    region,
    perm_table,
):
    slab = lax.axis_index("slab").astype(jnp.int32)
    core = lax.axis_index("blk").astype(jnp.int32)
    slabs = lax.axis_size("slab")
    planes, rows, width = pressure.shape
    cluster_size = near_blocks.shape[2]
    fault_cells = slip_rate.shape[0]
    clusters = fault_cells // cluster_size
    forward = [(i, i + 1) for i in range(slabs - 1)]
    backward = [(target, source) for source, target in forward]
    swap = [(0, 1), (1, 0)]
    chunks = row_chunks(rows)
    kinds = perm_table.shape[0]
    table = jnp.broadcast_to(jnp.pad(1.0 / perm_table, (0, 128 - kinds)), (8, 128))
    core_1 = core.reshape(1)
    valid = (slab > 0).astype(jnp.int32).reshape(1)
    slip = slip_rate.reshape(1, fault_cells)
    leak = leak_rate.reshape(1, fault_cells)

    *packed, edge, message = prepare(
        pressure, region, slip, col_basis, core_1, chunks, clusters, slabs
    )
    halos = [lax.ppermute(part, "slab", forward) for part in packed]
    edge = lax.ppermute(edge, "blk", swap)
    got = lax.all_to_all(message, "slab", 0, 0, tiled=True)

    sampled, source = cells(
        pressure, corner, fraction, slip, leak, (core * rows).reshape(1), 512
    )

    lows = [
        face_flux(halo, pressure, region, table, valid, start, size)
        for halo, (start, size) in zip(halos, chunks)
    ]
    highs = [lax.ppermute(low, "slab", backward) for low in lows]
    low = lows[0] if len(lows) == 1 else jnp.concatenate(lows, 0)
    rate = local_stencil(pressure, region, edge, source, low, table, core_1, 128)

    far = jnp.stack([far_col, far_row, far_rank])
    place = jnp.stack([core, slab])
    share = traction_share(got, slip, near_blocks, far_coupling, far, row_basis, place)
    shares = jnp.concatenate([share, sampled], 0)
    shares = shares + lax.ppermute(shares, "blk", swap)
    traction, fault_pressure = shares[0], shares[1]
    effective = normal_stress - fault_pressure
    state_rate = jnp.exp(-log_state) - slip_rate
    slip_accel = (traction - effective * friction_b * state_rate) / (
        effective * friction_a / slip_rate + 0.5
    )
    for high, (start, size) in zip(highs, chunks):
        rate = finish(rate, high, planes - 1, start, -1.0, size)
    return (slip_accel, state_rate, rate)


def solution(mesh):
    placed = (
        P("slab"),
        P("slab"),
        P("slab"),
        P("slab"),
        P("slab"),
        P("slab"),
        P(None, "slab"),
        P(None, "slab"),
        P(("slab", "blk"), None, None, None),
        P(None, "slab"),
        P(None, "slab"),
        P(("slab", "blk")),
        P(("slab", "blk")),
        P(("slab", "blk")),
        P(None, None, ("slab", "blk")),
        P("slab", "blk", None),
        P("slab", "blk", None),
        P(),
    )
    return jax.shard_map(
        shards,
        mesh=mesh,
        in_specs=placed,
        out_specs=(P("slab"), P("slab"), P("slab", "blk", None)),
        check_vma=False,
    )
```

profile of v0, /device:TPU:6, one launch (start us, length us, event | category | flops | bytes accessed | tf_op | source)
XLA Modules:
  0.0 65.6 jit_solution(11860582693743677040)
XLA Ops:
  0.6 2.8 %prepare.1 = (bf16[2,256,1024]{2,1,0:T(8,128)(2,1)}, f32[4,1024]{1,0:T(4,128)}, bf16[16,16,128]{2,1,0:T(8,128)(2,1)}) custom-call(s32[1]{0:T(128)} %bitcast.core_ref, f32[2,256,1024]{2,1,0:T(8,128)} %p_after.1, s32[2,256,1024]{2,1,0:T(8,128)} %k_after.1, f32[2,256,1024]{2,1,0:T(8,128)} %p_after.1, s32[2,256,1024]{2,1,0:T(8,128)} %k_after.1, ...), custom_call_target="tpu_custom_call" | custom-call | tf_op jit(solution)/shard_map/prepare/pallas_call | solution.py:78
  3.4 7.3 %all-to-all-start = ((bf16[16,16,128]{2,1,0:T(8,128)(2,1)}), bf16[16,16,128]{2,1,0:T(8,128)(2,1)S(1)}, u32[]{:S(2)}, u32[]{:S(2)}) async-start(bf16[16,16,128]{2,1,0:T(8,128)(2,1)} %get-tuple-element.8), calls=%async_computation | async-start | bytes 131072 | tf_op jit(solution)/shard_map/all_to_all | solution.py:446
  10.7 3.4 %collective-permute-start.1 = (bf16[2,256,1024]{2,1,0:T(8,128)(2,1)}, bf16[2,256,1024]{2,1,0:T(8,128)(2,1)S(1)}, u32[]{:S(2)}, u32[]{:S(2)}) collective-permute-start(bf16[2,256,1024]{2,1,0:T(8,128)(2,1)} %get-tuple-element.10), channel_id=1, source_target_pairs={{0,2},{2,4},{4,6},{6,8},{8,10},{10,12},{12,14},{14,16},{16,18},{18... | collective-permute-start | bytes 3145736 | tf_op jit(solution)/shard_map/ppermute | solution.py:444
  14.1 0.1 collective-permute-start.3
  14.1 0.0 copy-start.10
  14.2 0.0 copy-start.11
  14.2 0.0 copy-start.12
  14.2 14.4 %cells.1 = (f32[1,2048]{1,0:T(1,128)}, f32[2,256,1024]{2,1,0:T(8,128)}) custom-call(s32[1]{0:T(128)} %bitcast.6.start_ref, f32[2,256,1024]{2,1,0:T(8,128)} %p_after.1, s32[3,2048]{1,0:T(4,128)} %corner_ref.1, f32[3,2048]{1,0:T(4,128)} %fraction_ref.1, f32[1,2048]{1,0:T(1,128)} %bitcast.12, f32[1,2048]{1,0:T(1,128)} %bitcast.19), custom_call_target="tpu_custom_call" | custom-call | flops 6442450944 | bytes 4194304 | tf_op jit(solution)/shard_map/cells/pallas_call | solution.py:143
  28.6 0.6 pad_add_fusion.1.place_ref
  29.2 0.0 copy-done.10
  29.2 0.0 copy-done.11
  29.2 0.0 copy-done.12
  29.2 0.6 pad_add_fusion.far_ref
  29.8 0.0 copy-start.4
  29.8 0.0 copy-start.13
  29.8 0.0 all-to-all-done.got_ref
  29.8 0.0 copy-start.2
  29.9 0.6 copy-done.2
  30.5 4.5 %traction.1 = f32[1,2048]{1,0:T(1,128)} custom-call(s32[2]{0:T(128)} %pad_add_fusion.1.place_ref, bf16[16,16,128]{2,1,0:T(8,128)(2,1)} %copy-done.2, f32[1,2048]{1,0:T(1,128)} %bitcast.13, bf16[2,3,512,512]{3,2,1,0:T(8,128)(2,1)} %near_ref.1, bf16[24,24,1024]{2,1,0:T(8,128)(2,1)} %coupling_ref.1, s32[3,1024]{1,0:T(4,128)} %pad_add_fusion.far_ref, ...), custom_call_target="tpu_custom_call" | custom-call | tf_op jit(solution)/shard_map/traction/pallas_call | solution.py:394
  34.9 0.0 copy-done.4
  35.0 0.7 %pad_maximum_fusion = f32[2,2048]{1,0:T(2,128)S(1)} fusion(f32[1,2048]{1,0:T(1,128)S(1)} %copy-done.4, f32[1,2048]{1,0:T(1,128)} %traction.1), kind=kLoop, calls=%fused_computation.1 | loop fusion | flops 4096 | bytes 32768 | tf_op jit(solution)/shard_map/concatenate | solution.py:463
  35.7 0.5 collective-permute-start
  36.2 0.0 copy-done.13
  36.2 0.8 %collective-permute-done = f32[2,2048]{1,0:T(2,128)S(1)} collective-permute-done((f32[2,2048]{1,0:T(2,128)S(1)}, f32[2,2048]{1,0:T(2,128)S(1)}, u32[]{:S(2)}, u32[]{:S(2)}) %collective-permute-start) | collective-permute-done | bytes 16416 | tf_op jit(solution)/shard_map/ppermute | solution.py:464
  37.0 0.7 %fusion = f32[2,2048]{1,0:T(2,128)S(1)} fusion(f32[2,2048]{1,0:T(2,128)S(1)} %collective-permute-done, f32[1,2048]{1,0:T(1,128)S(1)} %copy-done.4, f32[1,2048]{1,0:T(1,128)} %traction.1), kind=kLoop, calls=%fused_computation.6 | loop fusion | flops 8192 | bytes 49152 | tf_op jit(solution)/shard_map/add | solution.py:464
  37.8 0.0 collective-permute-done.1.halo_ref
  37.8 0.0 copy-start
  37.8 0.6 broadcast_in_dim.3.table_ref
  38.4 0.4 copy-done
  38.8 0.0 copy-start.3
  38.8 0.0 copy-start.6
  38.8 0.0 copy-start.7
  38.8 0.0 copy-start.8
  38.8 0.0 copy-start.9
  38.8 5.4 %face.1.low_ref = bf16[256,1024]{1,0:T(8,128)(2,1)} custom-call(s32[1]{0:T(128)} %bitcast.10.valid_ref, f32[8,128]{1,0:T(8,128)} %broadcast_in_dim.3.table_ref, bf16[2,256,1024]{2,1,0:T(8,128)(2,1)} %copy-done, f32[2,256,1024]{2,1,0:T(8,128)} %p_after.1, s32[2,256,1024]{2,1,0:T(8,128)} %k_after.1), custom_call_target="tpu_custom_call" | custom-call | tf_op jit(solution)/shard_map/face/pallas_call | solution.py:296
  44.2 2.9 %collective-permute-start.2 = (bf16[256,1024]{1,0:T(8,128)(2,1)}, bf16[256,1024]{1,0:T(8,128)(2,1)S(1)}, u32[]{:S(2)}, u32[]{:S(2)}) collective-permute-start(bf16[256,1024]{1,0:T(8,128)(2,1)} %face.1.low_ref), channel_id=1, source_target_pairs={{2,0},{4,2},{6,4},{8,6},{10,8},{12,10},{14,12},{16,14},{18,16},{20... | collective-permute-start | bytes 1572872 | tf_op jit(solution)/shard_map/ppermute | solution.py:456
  47.1 0.0 copy-done.3
  47.1 0.0 copy-done.6
  47.2 0.0 copy-done.7
  47.2 0.0 copy-done.8
  47.2 0.0 copy-done.9
  47.2 0.6 add_divide_fusion
  47.8 0.0 collective-permute-done.3.edge_ref
  47.8 0.0 copy-start.5
  47.8 0.6 copy-done.5
  48.4 10.6 %stencil.1.acc_ref = f32[2,256,1024]{2,1,0:T(8,128)} custom-call(s32[1]{0:T(128)} %bitcast.core_ref, f32[8,128]{1,0:T(8,128)} %broadcast_in_dim.3.table_ref, f32[2,256,1024]{2,1,0:T(8,128)} %p_after.1, f32[2,256,1024]{2,1,0:T(8,128)} %p_after.1, f32[2,256,1024]{2,1,0:T(8,128)} %p_after.1, s32[2,256,1024]{2,1,0:T(8,128)} %k_after.1, ...), custom_call_target="tpu_custom_call", output_to_operand_aliasing={{}: (9, {})} | custom-call | flops 104857600 | bytes 8388608 | tf_op jit(solution)/shard_map/stencil/pallas_call | solution.py:255
  59.0 3.3 %collective-permute-done.2.flux_ref = bf16[256,1024]{1,0:T(8,128)(2,1)S(1)} collective-permute-done((bf16[256,1024]{1,0:T(8,128)(2,1)}, bf16[256,1024]{1,0:T(8,128)(2,1)S(1)}, u32[]{:S(2)}, u32[]{:S(2)}) %collective-permute-start.2) | collective-permute-done | bytes 524320 | tf_op jit(solution)/shard_map/ppermute | solution.py:456
  62.3 0.0 copy-start.1
  62.3 0.8 %copy-done.1 = bf16[256,1024]{1,0:T(8,128)(2,1)} copy-done((bf16[256,1024]{1,0:T(8,128)(2,1)}, bf16[256,1024]{1,0:T(8,128)(2,1)S(1)}, u32[]{:S(2)}) %copy-start.1) | copy-done | bytes 524312
  63.1 2.5 %finish.1 = f32[2,256,1024]{2,1,0:T(8,128)} custom-call(bf16[256,1024]{1,0:T(8,128)(2,1)} %copy-done.1, f32[2,256,1024]{2,1,0:T(8,128)} %stencil.1.acc_ref), custom_call_target="tpu_custom_call", output_to_operand_aliasing={{}: (1, {})} | custom-call | tf_op jit(solution)/shard_map/finish/pallas_call | solution.py:320
  (3 shorter events, 0.0 us)
Async XLA Ops:
  3.4 26.4 %all-to-all-start = ((bf16[16,16,128]{2,1,0:T(8,128)(2,1)}), bf16[16,16,128]{2,1,0:T(8,128)(2,1)S(1)}, u32[]{:S(2)}, u32[]{:S(2)}) async-start(bf16[16,16,128]{2,1,0:T(8,128)(2,1)} %get-tuple-element.8), calls=%async_computation | async-start | bytes 131072 | tf_op jit(solution)/shard_map/all_to_all | solution.py:446
  10.7 27.1 %collective-permute-start.1 = (bf16[2,256,1024]{2,1,0:T(8,128)(2,1)}, bf16[2,256,1024]{2,1,0:T(8,128)(2,1)S(1)}, u32[]{:S(2)}, u32[]{:S(2)}) collective-permute-start(bf16[2,256,1024]{2,1,0:T(8,128)(2,1)} %get-tuple-element.10), channel_id=1, source_target_pairs={{0,2},{2,4},{4,6},{6,8},{8,10},{10,12},{12,14},{14,16},{16,18},{18... | collective-permute-start | bytes 3145736 | tf_op jit(solution)/shard_map/ppermute | solution.py:444
  14.1 33.7 %collective-permute-start.3 = (f32[4,1024]{1,0:T(4,128)}, f32[4,1024]{1,0:T(4,128)S(1)}, u32[]{:S(2)}, u32[]{:S(2)}) collective-permute-start(f32[4,1024]{1,0:T(4,128)} %get-tuple-element.11), channel_id=1, source_target_pairs={{0,1},{1,0},{2,3},{3,2},{4,5},{5,4},{6,7},{7,6},{8,9},{9,8},{10,11... | collective-permute-start | bytes 49160 | tf_op jit(solution)/shard_map/ppermute | solution.py:445
  14.1 15.1 %copy-start.10 = (s32[1024]{0:T(1024)S(1)}, s32[1024]{0:T(1024)}, u32[]{:S(2)}) copy-start(s32[1024]{0:T(1024)} %param.31) | copy-start | bytes 12292
  14.2 15.1 %copy-start.11 = (s32[1024]{0:T(1024)S(1)}, s32[1024]{0:T(1024)}, u32[]{:S(2)}) copy-start(s32[1024]{0:T(1024)} %param.29) | copy-start | bytes 12292
  14.2 15.1 %copy-start.12 = (s32[1024]{0:T(1024)S(1)}, s32[1024]{0:T(1024)}, u32[]{:S(2)}) copy-start(s32[1024]{0:T(1024)} %param.30) | copy-start | bytes 12292
  29.8 5.1 %copy-start.4 = (f32[1,2048]{1,0:T(1,128)S(1)}, f32[1,2048]{1,0:T(1,128)}, u32[]{:S(2)}) copy-start(f32[1,2048]{1,0:T(1,128)} %get-tuple-element.9) | copy-start | bytes 24580
  29.8 6.4 %copy-start.13 = (f32[16]{0:T(128)S(1)}, f32[16]{0:T(128)}, u32[]{:S(2)}) copy-start(f32[16]{0:T(128)} %param.35) | copy-start | bytes 196
  29.8 0.6 copy-start.2
  35.7 1.4 %collective-permute-start = (f32[2,2048]{1,0:T(2,128)S(1)}, f32[2,2048]{1,0:T(2,128)S(1)}, u32[]{:S(2)}, u32[]{:S(2)}) collective-permute-start(f32[2,2048]{1,0:T(2,128)S(1)} %pad_maximum_fusion), channel_id=1, source_target_pairs={{0,1},{1,0},{2,3},{3,2},{4,5},{5,4},{6,7},{7,6},{8,9},{9,8},{10,11... | collective-permute-start | bytes 49160 | tf_op jit(solution)/shard_map/ppermute | solution.py:464
  37.8 1.0 %copy-start = (bf16[2,256,1024]{2,1,0:T(8,128)(2,1)}, bf16[2,256,1024]{2,1,0:T(8,128)(2,1)S(1)}, u32[]{:S(2)}) copy-start(bf16[2,256,1024]{2,1,0:T(8,128)(2,1)S(1)} %collective-permute-done.1.halo_ref) | copy-start | bytes 3145732
  38.8 8.4 %copy-start.3 = (f32[2048]{0:T(1024)S(1)}, f32[2048]{0:T(1024)}, u32[]{:S(2)}) copy-start(f32[2048]{0:T(1024)} %param.18) | copy-start | bytes 24580
  38.8 8.4 %copy-start.6 = (f32[2048]{0:T(1024)S(1)}, f32[2048]{0:T(1024)}, u32[]{:S(2)}) copy-start(f32[2048]{0:T(1024)} %param.20) | copy-start | bytes 24580
  38.8 8.4 %copy-start.7 = (f32[2048]{0:T(1024)S(1)}, f32[2048]{0:T(1024)}, u32[]{:S(2)}) copy-start(f32[2048]{0:T(1024)} %param.21) | copy-start | bytes 24580
  38.8 8.4 %copy-start.8 = (f32[2048]{0:T(1024)S(1)}, f32[2048]{0:T(1024)}, u32[]{:S(2)}) copy-start(f32[2048]{0:T(1024)} %param.22) | copy-start | bytes 24580
  38.8 8.4 %copy-start.9 = (f32[2048]{0:T(1024)S(1)}, f32[2048]{0:T(1024)}, u32[]{:S(2)}) copy-start(f32[2048]{0:T(1024)} %param.19) | copy-start | bytes 24580
  44.2 18.1 %collective-permute-start.2 = (bf16[256,1024]{1,0:T(8,128)(2,1)}, bf16[256,1024]{1,0:T(8,128)(2,1)S(1)}, u32[]{:S(2)}, u32[]{:S(2)}) collective-permute-start(bf16[256,1024]{1,0:T(8,128)(2,1)} %face.1.low_ref), channel_id=1, source_target_pairs={{2,0},{4,2},{6,4},{8,6},{10,8},{12,10},{14,12},{16,14},{18,16},{20... | collective-permute-start | bytes 1572872 | tf_op jit(solution)/shard_map/ppermute | solution.py:456
  47.8 0.6 copy-start.5
  62.3 0.8 %copy-start.1 = (bf16[256,1024]{1,0:T(8,128)(2,1)}, bf16[256,1024]{1,0:T(8,128)(2,1)S(1)}, u32[]{:S(2)}) copy-start(bf16[256,1024]{1,0:T(8,128)(2,1)S(1)} %collective-permute-done.2.flux_ref) | copy-start | bytes 1572868
where the time goes:
time: 66 us; the launch traced here: 65.6 us
  Pallas kernels  40.2 us (61%)
  starting transfers between devices  14.1 us (21%)
  waiting for transfers between devices  4.1 us (6%)
  other arithmetic  3.28 us (5%)
  local copies, waits for them, and re-layouts  3.07 us (5%)
  between operations  0.79 us (1%)
    pallas_call x1, Pallas kernels, cells(): pl.pallas_call(cells_kernel, grid=(count // block,), in_specs=[pl.BlockSp...  14.4 us
    pallas_call x1, Pallas kernels, local_stencil(): pl.pallas_call(stencil_kernel, grid=(rows // block,), in_specs=[smem, ful...  10.6 us
    all_to_all x1, starting transfers between devices, shards(): got = lax.all_to_all(message, 'slab', 0, 0, tiled=True)  7.25 us
    pallas_call x1, Pallas kernels, face_flux(): pl.pallas_call(face_kernel, grid=(size // block,), in_specs=[smem, pl.Blo...  5.42 us
    pallas_call x1, Pallas kernels, traction_share(): pl.pallas_call(functools.partial(traction_kernel, half_rows=near_blocks.s...  4.48 us
    ppermute x1, starting transfers between devices, shards(): halos = [lax.ppermute(part, 'slab', forward) for part in packed]  3.36 us
    ppermute x1, waiting for transfers between devices, shards(): highs = [lax.ppermute(low, 'slab', backward) for low in lows]  3.27 us
    ppermute x1, starting transfers between devices, shards(): highs = [lax.ppermute(low, 'slab', backward) for low in lows]  2.88 us
  transfers between devices with their start and end apart: 5, of which 2 were waited for; matrix products, arithmetic and copies ran while one was open for 6% of the time, Pallas kernels for 53%

commit v1 on v0

v1 whole, which is shorter than its diff:
```python
import functools

import jax
import jax.numpy as jnp
from jax import lax
from jax.experimental import pallas as pl
from jax.experimental.pallas import tpu as pltpu
from jax.sharding import PartitionSpec as P


VMEM = pltpu.MemorySpace.VMEM
SMEM = pltpu.MemorySpace.SMEM
UNROLL = 32
PARTS = (4, 4)
VMEM_OUT = pltpu.VMEM


def row_parts(rows):
    sizes = [rows * part // sum(PARTS) for part in PARTS]
    return [(sum(sizes[:i]), size) for i, size in enumerate(sizes)]


def params(megabytes):
    return pltpu.CompilerParams(vmem_limit_bytes=megabytes << 20)


def in_hbm(x):
    return pltpu.with_memory_space_constraint(x, pltpu.MemorySpace.HBM)


def make_table(values_ref):
    lane = lax.broadcasted_iota(jnp.int32, (8, 128), 1)
    table = jnp.ones((8, 128), jnp.float32)
    for i in range(values_ref.shape[0]):
        table = jnp.where(lane == i, values_ref[i], table)
    return 1.0 / table


def lookup(table, index):
    height, width = index.shape
    table = jnp.concatenate([table] * (height // 8), axis=0)
    parts = [
        jnp.take_along_axis(table, index[:, at : at + 128], axis=1) for at in range(0, width, 128)
    ]
    return jnp.concatenate(parts, axis=1)


def prepare_kernel(
    clusters, core_ref, slab_ref, p_hbm, k_hbm, slip_hbm, basis_hbm, halo_ref, edge_ref, message_ref, p_ref, k_ref,
    p_edge, k_edge, slip_ref, basis_ref, sems,
):
    f32, bf16 = jnp.float32, jnp.bfloat16
    planes, rows = p_hbm.shape[0], p_hbm.shape[1]
    low = core_ref[0] != 0
    at = pl.multiple_of((1 - core_ref[0]) * (rows - 8), 8)
    parts = [pl.ds(i * (rows // 2), rows // 2) for i in range(2)]
    moves = [
        (source.at[planes - 1, part], target.at[part])
        for part in parts
        for source, target in ((p_hbm, p_ref), (k_hbm, k_ref))
    ]
    moves += [
        (p_hbm.at[:, pl.ds(at, 8)], p_edge),
        (k_hbm.at[:, pl.ds(at, 8)], k_edge),
        (slip_hbm, slip_ref),
        (basis_hbm, basis_ref),
    ]
    copies = [pltpu.make_async_copy(*move, sems.at[i]) for i, move in enumerate(moves)]
    for copy in copies:
        copy.start()
    for i, part in enumerate(parts):
        copies[2 * i].wait()
        halo_ref[0, part, :] = p_ref[part, :].astype(bf16)
        copies[2 * i + 1].wait()
        halo_ref[1, part, :] = k_ref[part, :].astype(f32).astype(bf16)
    for copy in copies[4:]:
        copy.wait()
    for plane in range(planes):
        block, kind = p_edge[plane], k_edge[plane].astype(f32)
        edge_ref[plane : plane + 1, :] = jnp.where(low, block[0:1, :], block[7:8, :])
        edge_ref[planes + plane : planes + plane + 1, :] = jnp.where(low, kind[0:1, :], kind[7:8, :])
    cells = slip_ref.shape[1]
    size = cells // clusters
    slip = slip_ref[...].astype(bf16).astype(f32)
    lines = [slip[:, at : at + 128] for at in range(0, size, 128)]
    lines += [slip[:, at : at + 128] for at in range(cells - size, cells, 128)]
    rank = basis_ref.shape[0]
    for cluster in range(clusters):
        part = slip[:, cluster * size : (cluster + 1) * size].astype(bf16)
        moment = lax.dot_general(
            jnp.broadcast_to(part, (16, size)),
            basis_ref[:, cluster * size : (cluster + 1) * size],
            (((1,), (1,)), ((), ())),
            preferred_element_type=f32,
        )[0:1, :]
        lines.append(jnp.concatenate([moment, jnp.zeros((1, 128 - rank), f32)], axis=1))
    height = message_ref.shape[1]
    lines.append(jnp.zeros((height - len(lines), 128), f32))
    message = jnp.concatenate(lines, axis=0).astype(bf16)
    for slab in range(message_ref.shape[0]):
        message_ref[slab] = message


def prepare(core, slab, pressure, region, slip, basis, clusters, slabs):
    planes, rows, width = pressure.shape
    cells = slip.shape[1]
    lines = 2 * (cells // clusters // 128) + clusters
    height = -(-lines // 16) * 16
    vmem, smem = pl.BlockSpec(memory_space=VMEM), pl.BlockSpec(memory_space=SMEM)
    return pl.pallas_call(
        functools.partial(prepare_kernel, clusters),
        in_specs=[smem] * 2 + [pl.BlockSpec(memory_space=pl.ANY)] * 4,
        out_specs=[vmem] * 3,
        out_shape=[
            VMEM_OUT((2, rows, width), jnp.bfloat16),
            VMEM_OUT((2 * planes, width), jnp.float32),
            VMEM_OUT((slabs, height, 128), jnp.bfloat16),
        ],
        scratch_shapes=[
            pltpu.VMEM((rows, width), pressure.dtype),
            pltpu.VMEM((rows, width), region.dtype),
            pltpu.VMEM((planes, 8, width), pressure.dtype),
            pltpu.VMEM((planes, 8, width), region.dtype),
            pltpu.VMEM(slip.shape, slip.dtype),
            pltpu.VMEM(basis.shape, basis.dtype),
            pltpu.SemaphoreType.DMA((8,)),
        ],
        name="prepare",
    )(core, slab, pressure, region, slip, basis)


def cells_kernel(
    core_ref, p_hbm, k_hbm, corner_ref, fraction_ref, slip_ref, leak_ref, sampled_ref, source_ref, p_ref, k_ref,
    field, sems, *slots, block
):
    _, rows, width = p_ref.shape
    f32, bf16, i16 = jnp.float32, jnp.bfloat16, jnp.int16
    steps = corner_ref.shape[1] // block
    iota = lax.broadcasted_iota(jnp.int32, (16, block), 0).astype(i16)
    iota_y = lax.broadcasted_iota(jnp.int32, (rows, block), 0)
    zero = jnp.float32(0.0)
    zeros = jnp.zeros((16, block), bf16)
    p_copy = pltpu.make_async_copy(p_hbm, p_ref, sems.at[0])
    k_copy = pltpu.make_async_copy(k_hbm, k_ref, sems.at[1])
    p_copy.start()

    def spread_rows(x, kind):
        return jnp.broadcast_to(x, (16, block)).astype(kind)

    def build(step, z_hi, z_lo, weight, scaled):
        at = slice(step * block, (step + 1) * block)
        frac_x, frac_y, frac_z = (fraction_ref[i : i + 1, at] for i in range(3))
        at_y = corner_ref[1:2, at] - core_ref[0] * rows
        at_z = spread_rows(corner_ref[2:3, at], i16)
        next_z = at_z + jnp.int16(1)
        low_z = 1.0 - frac_z
        low_hi, high_hi = spread_rows(low_z, bf16), spread_rows(frac_z, bf16)
        low_lo = (low_z - low_hi.astype(f32)).astype(bf16)
        high_lo = (frac_z - high_hi.astype(f32)).astype(bf16)
        for row in range(0, width, 16):
            here = iota == at_z - jnp.int16(row)
            above = iota == next_z - jnp.int16(row)
            z_hi[row : row + 16, :] = jnp.where(here, low_hi, jnp.where(above, high_hi, zeros))
            z_lo[row : row + 16, :] = jnp.where(here, low_lo, jnp.where(above, high_lo, zeros))
        weight_y = jnp.where(
            iota_y == at_y, 1.0 - frac_y, jnp.where(iota_y == at_y + 1, frac_y, zero)
        )
        weight[...] = weight_y
        flow = slip_ref[:, at] * leak_ref[:, at]
        for plane in range(2):
            weight_x = frac_x if plane else 1.0 - frac_x
            scaled[plane] = (weight_y * (weight_x * flow)).astype(bf16)

    def apply(step, z_hi, z_lo, weight, scaled):
        at = slice(step * block, (step + 1) * block)
        frac_x = fraction_ref[0:1, at]
        total = jnp.zeros((1, block), f32)
        for plane in range(2):
            weight_x = frac_x if plane else 1.0 - frac_x
            along = jnp.dot(field[plane], z_hi[...], preferred_element_type=f32)
            total = total + weight_x * jnp.sum(weight[...] * along, axis=0, keepdims=True)
            dims = (((1,), (1,)), ((), ()))
            spread = lax.dot_general(scaled[plane], z_hi[...], dims, preferred_element_type=f32)
            spread = spread + lax.dot_general(scaled[plane], z_lo[...], dims, preferred_element_type=f32)
            source_ref[plane] = spread if step == 0 else source_ref[plane] + spread
        sampled_ref[:, at] = total

    half = len(slots) // 2
    pair = (slots[:half], slots[half:])
    build(0, *pair[0])
    build(1, *pair[1])
    p_copy.wait()
    k_copy.start()
    field[...] = p_ref[...].astype(bf16)
    for step in range(steps):
        apply(step, *pair[step % 2])
        if step + 2 < steps:
            build(step + 2, *pair[step % 2])
    k_copy.wait()


def cells(core, pressure, region, corner, fraction, slip, leak, block):
    planes, rows, width = pressure.shape
    count = corner.shape[1]
    vmem, smem = pl.BlockSpec(memory_space=VMEM), pl.BlockSpec(memory_space=SMEM)
    hbm = pl.BlockSpec(memory_space=pl.ANY)
    slot = [
        pltpu.VMEM((width, block), jnp.bfloat16),
        pltpu.VMEM((width, block), jnp.bfloat16),
        pltpu.VMEM((rows, block), jnp.float32),
        pltpu.VMEM((planes, rows, block), jnp.bfloat16),
    ]
    return pl.pallas_call(
        functools.partial(cells_kernel, block=block),
        in_specs=[smem, hbm, hbm] + [vmem] * 4,
        out_specs=[vmem] * 4,
        out_shape=[
            VMEM_OUT((1, count), jnp.float32),
            VMEM_OUT(pressure.shape, jnp.float32),
            VMEM_OUT(pressure.shape, pressure.dtype),
            VMEM_OUT(region.shape, region.dtype),
        ],
        scratch_shapes=[pltpu.VMEM(pressure.shape, jnp.bfloat16), pltpu.SemaphoreType.DMA((2,))] + slot + slot,
        compiler_params=params(20),
        cost_estimate=pl.CostEstimate(
            flops=6 * planes * rows * width * count, bytes_accessed=8 * pressure.size, transcendentals=0
        ),
        name="cells",
    )(core, in_hbm(pressure), in_hbm(region), corner, fraction, slip, leak)


def stencil_kernel(
    core_ref, perm_ref, p_ref, k_ref, edge_ref, source_ref, out_ref, pad_p, pad_r
):
    planes, rows, width = p_ref.shape
    f32 = jnp.float32
    far = jnp.float32(jnp.inf)
    core = core_ref[0]
    table = make_table(perm_ref)
    outside = jnp.full((8, width), far, f32)
    for plane in range(planes):
        edge_p = jnp.broadcast_to(edge_ref[plane : plane + 1, :], (8, width))
        edge_k = edge_ref[planes + plane : planes + plane + 1, :].astype(jnp.int32)
        edge_r = lookup(table, jnp.broadcast_to(edge_k, (8, width)))
        pad_p[plane, 0:8, :] = edge_p
        pad_p[plane, rows + 8 : rows + 16, :] = edge_p
        pad_r[plane, 0:8, :] = jnp.where(core == 0, outside, edge_r)
        pad_r[plane, rows + 8 : rows + 16, :] = jnp.where(core == 0, edge_r, outside)

    def fill(s, carry):
        at = pl.multiple_of(s * 32, 8)
        to = pl.multiple_of(s * 32 + 8, 8)
        for plane in range(planes):
            pad_p[plane, pl.ds(to, 32), :] = p_ref[plane, pl.ds(at, 32), :]
            pad_r[plane, pl.ds(to, 32), :] = lookup(table, k_ref[plane, pl.ds(at, 32), :])
        return carry

    lax.fori_loop(0, rows // 32, fill, 0)
    lane = lax.broadcasted_iota(jnp.int32, (8, width), 1)
    sub = lax.broadcasted_iota(jnp.int32, (8, width), 0)

    def face(p, r, p_next, r_next):
        return 2.0 / (r + r_next) * (p_next - p)

    def y_face(plane, at):
        p, r = pad_p[plane, pl.ds(at, 8), :], pad_r[plane, pl.ds(at, 8), :]
        after = pl.multiple_of(at + 8, 8)
        pn, rn = pad_p[plane, pl.ds(after, 8), :], pad_r[plane, pl.ds(after, 8), :]
        pn = pltpu.roll(jnp.where(sub == 0, pn, p), 7, 0)
        rn = pltpu.roll(jnp.where(sub == 0, rn, r), 7, 0)
        return p, r, face(p, r, pn, rn)

    def strip(to, carry):
        at = pl.multiple_of(to + 8, 8)
        after = []
        sums, ps, rs = [], [], []
        for plane in range(planes):
            p, r, fy = y_face(plane, at)
            below = pltpu.roll(jnp.where(sub == 7, carry[plane], fy), 1, 0)
            after.append(fy)
            pz = pltpu.roll(p, width - 1, 1)
            rz = jnp.where(lane == width - 1, far, pltpu.roll(r, width - 1, 1))
            fz = face(p, r, pz, rz)
            sums.append(fy - below + (fz - pltpu.roll(fz, 1, 1)))
            ps.append(p)
            rs.append(r)
        for plane in range(planes - 1):
            fx = face(ps[plane], rs[plane], ps[plane + 1], rs[plane + 1])
            sums[plane] = sums[plane] + fx
            sums[plane + 1] = sums[plane + 1] - fx
        for plane in range(planes):
            out_ref[plane, pl.ds(to, 8), :] = source_ref[plane, pl.ds(to, 8), :] + sums[plane]
        return tuple(after)

    def body(s, carry):
        for at in range(0, UNROLL, 8):
            carry = strip(pl.multiple_of(s * UNROLL + at, 8), carry)
        return carry

    first = tuple(y_face(plane, 0)[2] for plane in range(planes))
    lax.fori_loop(0, rows // UNROLL, body, first)


def local_stencil(core, perm, pressure, region, edge, source):
    planes, rows, width = pressure.shape
    vmem, smem = pl.BlockSpec(memory_space=VMEM), pl.BlockSpec(memory_space=SMEM)
    return pl.pallas_call(
        stencil_kernel,
        in_specs=[smem, smem] + [vmem] * 4,
        out_specs=vmem,
        out_shape=VMEM_OUT(pressure.shape, jnp.float32),
        scratch_shapes=[pltpu.VMEM((planes, rows + 16, width), jnp.float32)] * 2,
        input_output_aliases={5: 0},
        compiler_params=params(20),
        cost_estimate=pl.CostEstimate(
            flops=200 * pressure.size, bytes_accessed=16 * pressure.size, transcendentals=0
        ),
        name="stencil",
    )(core, perm, pressure, region, edge, source)


def face_kernel(start, slab_ref, perm_ref, halo_ref, p_ref, region_ref, out_ref):
    valid = slab_ref[0] > 0
    far = jnp.float32(jnp.inf)
    table = make_table(perm_ref)

    def body(s, carry):
        at = pl.multiple_of(s * 32, 32)
        rows, own = pl.ds(at, 32), pl.ds(pl.multiple_of(start + at, 32), 32)
        other_p = halo_ref[0, own, :].astype(jnp.float32)
        other_r = lookup(table, halo_ref[1, own, :].astype(jnp.float32).astype(jnp.int32))
        other_r = jnp.where(valid, other_r, far)
        r = lookup(table, region_ref[0, own, :])
        flux = 2.0 / (r + other_r) * (other_p - p_ref[0, own, :])
        out_ref[rows, :] = flux.astype(jnp.bfloat16)
        return carry

    lax.fori_loop(0, out_ref.shape[0] // 32, body, 0)


def face_flux(slab, perm, halo, pressure, region, start, size):
    vmem, smem = pl.BlockSpec(memory_space=VMEM), pl.BlockSpec(memory_space=SMEM)
    return pl.pallas_call(
        functools.partial(face_kernel, start),
        in_specs=[smem, smem] + [vmem] * 3,
        out_specs=vmem,
        out_shape=VMEM_OUT((size, halo.shape[2]), jnp.bfloat16),
        compiler_params=params(8),
        name="face",
    )(slab, perm, halo, pressure, region)


def finish_kernel(
    acc_ref, mine_ref, theirs_ref, slip_ref, state_ref, a_ref, b_ref, normal_ref, *rest
):
    *highs, _, out_ref, accel_ref, rate_ref, final, sems = rest
    plane, rows = acc_ref.shape[0] - 1, acc_ref.shape[1]
    copies = []
    for i, (start, size) in enumerate(row_parts(rows)):
        part = pl.ds(start, size)
        final[part, :] = acc_ref[plane, part, :] - highs[i][...].astype(jnp.float32)
        copy = pltpu.make_async_copy(final.at[part], out_ref.at[plane, part], sems.at[i])
        copy.start()
        copies.append(copy)
    shares = mine_ref[...] + theirs_ref[...]
    slip = slip_ref[...]
    effective = normal_ref[...] - shares[1:2, :]
    change = jnp.exp(-state_ref[...]) - slip
    accel_ref[...] = (shares[0:1, :] - effective * b_ref[...] * change) / (
        effective * a_ref[...] / slip + 0.5
    )
    rate_ref[...] = change
    for copy in copies:
        copy.wait()


def finish(acc, *cell_args, highs, rate):
    count = cell_args[-1].shape[1]
    vmem, hbm = pl.BlockSpec(memory_space=VMEM), pl.BlockSpec(memory_space=pl.ANY)
    line = jax.ShapeDtypeStruct((1, count), jnp.float32)
    return pl.pallas_call(
        finish_kernel,
        in_specs=[vmem] * (8 + len(highs)) + [hbm],
        out_specs=[hbm, vmem, vmem],
        out_shape=[jax.ShapeDtypeStruct(acc.shape, jnp.float32), line, line],
        scratch_shapes=[pltpu.VMEM(acc.shape[1:], jnp.float32), pltpu.SemaphoreType.DMA((len(highs),))],
        input_output_aliases={8 + len(highs): 0},
        compiler_params=params(8),
        name="finish",
    )(acc, *cell_args, *highs, rate)


def traction_kernel(
    core_ref, slab_ref, got_ref, sampled_ref, slip_ref, near_hbm, coupling_hbm, row_ref, col_ref, rank_ref, basis_hbm,
    acc_ref, *rest, half_rows
):
    lows = rest[:-8]
    out_ref, rate_hbm, near_ref, coupling_ref, basis_ref, final, sems, final_sems = rest[-8:]
    moves = ((coupling_hbm, coupling_ref), (basis_hbm, basis_ref), (near_hbm, near_ref))
    coupling_copy, basis_copy, near_copy = (
        pltpu.make_async_copy(*move, sems.at[i]) for i, move in enumerate(moves)
    )
    coupling_copy.start()
    basis_copy.start()
    near_copy.start()
    final_copies = []
    for i, (start, size) in enumerate(row_parts(acc_ref.shape[1])):
        part = pl.ds(start, size)
        final[part, :] = acc_ref[0, part, :] + lows[i][...].astype(jnp.float32)
        copy = pltpu.make_async_copy(final.at[part], rate_hbm.at[0, part], final_sems.at[i])
        copy.start()
        final_copies.append(copy)
    f32, bf16 = jnp.float32, jnp.bfloat16
    core, slab = core_ref[0], slab_ref[0]
    slabs = got_ref.shape[0]
    rank, cells = basis_ref.shape
    size = near_ref.shape[2]
    clusters = cells // size
    per = size // 128
    slots = row_ref.shape[1]

    cols, rows, ranks = col_ref[...], row_ref[...], rank_ref[...]
    owner, member = cols // clusters, cols % clusters
    slab_iota = lax.broadcasted_iota(jnp.int32, (slabs, slots), 0)
    pick = (slab_iota == owner).astype(f32).astype(bf16)
    picked = jnp.zeros((128, slots), f32)
    for cluster in range(clusters):
        sent = got_ref[:, 2 * per + cluster, :]
        chosen = lax.dot_general(sent, pick, (((0,), (0,)), ((), ())), preferred_element_type=f32)
        picked = jnp.where(member == cluster, chosen, picked)
    rank_iota = lax.broadcasted_iota(jnp.int32, (rank, slots), 0)
    masked = jnp.where(rank_iota < ranks, picked[:rank, :], jnp.float32(0.0))
    coupling_copy.wait()
    lines = []
    for a in range(rank):
        lines.append(jnp.sum(coupling_ref[a].astype(f32) * masked, axis=0, keepdims=True))
    block = jnp.concatenate(lines, axis=0)
    basis_copy.wait()
    far = []
    for cluster in range(clusters):
        total = jnp.sum(jnp.where(rows == cluster, block, jnp.float32(0.0)), axis=1, keepdims=True)
        basis = basis_ref[:, cluster * size : (cluster + 1) * size].astype(f32)
        far.append(jnp.sum(basis * total, axis=0, keepdims=True))

    def line(slab_at, row):
        parts = [got_ref[pl.ds(slab_at, 1), row + i, :].astype(f32) for i in range(per)]
        return jnp.concatenate(parts, axis=1)

    zero = jnp.zeros((1, size), f32)
    before = jnp.where(slab > 0, line(jnp.maximum(slab - 1, 0), per), zero)
    after = jnp.where(slab < slabs - 1, line(jnp.minimum(slab + 1, slabs - 1), 0), zero)
    slip = slip_ref[...].astype(bf16).astype(f32)
    extended = [before] + [slip[:, c * size : (c + 1) * size] for c in range(clusters)] + [after]
    near_copy.wait()
    near = []
    for i in range(half_rows):
        total = jnp.zeros((16, size), f32)
        for j in range(3):
            source = jnp.where(core == 0, extended[i + j], extended[half_rows + i + j])
            total = total + lax.dot_general(
                jnp.broadcast_to(source, (16, size)).astype(bf16),
                near_ref[i, j],
                (((1,), (1,)), ((), ())),
                preferred_element_type=f32,
            )
        near.append(total[0:1, :])
    for cluster in range(clusters):
        mine = (cluster // half_rows) == core
        out_ref[0:1, cluster * size : (cluster + 1) * size] = far[cluster] + jnp.where(
            mine, near[cluster % half_rows], zero
        )
    out_ref[1:2, :] = sampled_ref[...]
    for copy in final_copies:
        copy.wait()


def traction_share(core, slab, got, sampled, slip, near_blocks, coupling, rows, cols, ranks, basis, acc, lows):
    vmem, smem = pl.BlockSpec(memory_space=VMEM), pl.BlockSpec(memory_space=SMEM)
    hbm = pl.BlockSpec(memory_space=pl.ANY)
    return pl.pallas_call(
        functools.partial(traction_kernel, half_rows=near_blocks.shape[0]),
        in_specs=[smem] * 2 + [vmem] * 3 + [hbm] * 2 + [vmem] * 3 + [hbm] + [vmem] * (1 + len(lows)),
        out_specs=[vmem, hbm],
        out_shape=[
            VMEM_OUT((2, slip.shape[1]), jnp.float32),
            jax.ShapeDtypeStruct(acc.shape, jnp.float32),
        ],
        scratch_shapes=[
            pltpu.VMEM(near_blocks.shape, near_blocks.dtype),
            pltpu.VMEM(coupling.shape, coupling.dtype),
            pltpu.VMEM(basis.shape, basis.dtype),
            pltpu.VMEM(acc.shape[1:], acc.dtype),
            pltpu.SemaphoreType.DMA((3,)),
            pltpu.SemaphoreType.DMA((len(lows),)),
        ],
        compiler_params=params(16),
        name="traction",
    )(
        core, slab, got, sampled, slip, in_hbm(near_blocks), in_hbm(coupling), rows, cols, ranks, in_hbm(basis),
        acc, *lows,
    )


def shards(
    slip_rate,
    log_state,
    friction_a,
    friction_b,
    normal_stress,
    leak_rate,
    corner,
    fraction,
    near_blocks,
    row_basis,
    col_basis,
    far_row,
    far_col,
    far_rank,
    far_coupling,
    pressure,
    region,
    perm_table,
):
    slab = lax.axis_index("slab").astype(jnp.int32)
    core = lax.axis_index("blk").astype(jnp.int32)
    slabs = lax.axis_size("slab")
    _, rows, _ = pressure.shape
    cluster_size = near_blocks.shape[2]
    fault_cells = slip_rate.shape[0]
    clusters = fault_cells // cluster_size
    forward = [(i, i + 1) for i in range(slabs - 1)]
    backward = [(target, source) for source, target in forward]
    swap = [(0, 1), (1, 0)]
    core, slab = core.reshape(1), slab.reshape(1)
    line = lambda x: x.reshape(1, -1)
    slip = line(slip_rate)
    p_in, k_in = in_hbm(pressure), in_hbm(region)

    halo, edge, message = prepare(
        core, slab, p_in, k_in, in_hbm(slip), in_hbm(col_basis), clusters, slabs
    )
    halo = lax.ppermute(halo, "slab", forward)
    got = lax.all_to_all(message, "slab", 0, 0, tiled=True)
    edge = lax.ppermute(edge, "blk", swap)

    sampled, source, p, k = cells(
        core, pressure, region, corner, fraction, slip, line(leak_rate), 512
    )
    acc = local_stencil(core, perm_table, p, k, edge, source)
    lows, highs = [], []
    for start, size in row_parts(rows):
        low = face_flux(slab, perm_table, halo, p, k, start, size)
        highs.append(lax.ppermute(low, "slab", backward))
        lows.append(low)

    got, acc = lax.optimization_barrier((got, acc, *lows))[:2]
    shares, rate = traction_share(
        core,
        slab,
        got,
        sampled,
        slip,
        near_blocks,
        far_coupling,
        line(far_row),
        line(far_col),
        line(far_rank),
        row_basis,
        acc,
        lows,
    )
    others = lax.ppermute(shares, "blk", swap)
    rate, accel, change = finish(
        acc,
        shares,
        others,
        slip,
        line(log_state),
        line(friction_a),
        line(friction_b),
        line(normal_stress),
        highs=highs,
        rate=rate,
    )
    return (accel.reshape(-1), change.reshape(-1), rate)


def solution(mesh):
    placed = (
        P("slab"),
        P("slab"),
        P("slab"),
        P("slab"),
        P("slab"),
        P("slab"),
        P(None, "slab"),
        P(None, "slab"),
        P(("slab", "blk"), None, None, None),
        P(None, "slab"),
        P(None, "slab"),
        P(("slab", "blk")),
        P(("slab", "blk")),
        P(("slab", "blk")),
        P(None, None, ("slab", "blk")),
        P("slab", "blk", None),
        P("slab", "blk", None),
        P(),
    )

    return jax.shard_map(
        shards,
        mesh=mesh,
        in_specs=placed,
        out_specs=(P("slab"), P("slab"), P("slab", "blk", None)),
        check_vma=False,
    )
```

time: 66 us -> 65.8 us (level)
  the two profiles are of different devices: /device:TPU:6 before, /device:TPU:0 now
where the time goes in v1:
time: 65.8 us; the launch traced here: 65.4 us
  Pallas kernels  25.6 us (39%)
  starting transfers between devices  19.8 us (30%)
  waiting for transfers between devices  15.9 us (24%)
  local copies, waits for them, and re-layouts  3.25 us (5%)
  between operations  0.92 us (1%)
    ppermute x1, waiting for transfers between devices, shards(): halo = lax.ppermute(halo, 'slab', forward)  13.7 us
    all_to_all x1, starting transfers between devices, shards(): got = lax.all_to_all(message, 'slab', 0, 0, tiled=True)  11.9 us
    pallas_call x1, Pallas kernels, cells(): pl.pallas_call(functools.partial(cells_kernel, block=block), in_specs=[sm...  8.55 us
    pallas_call x1, Pallas kernels, local_stencil(): pl.pallas_call(stencil_kernel, in_specs=[smem, smem] + [vmem] * 4, out_sp...  6.08 us
    ppermute x1, starting transfers between devices, shards(): halo = lax.ppermute(halo, 'slab', forward)  4.94 us
    pallas_call x1, Pallas kernels, traction_share(): pl.pallas_call(functools.partial(traction_kernel, half_rows=near_blocks.s...  3.65 us
    unnamed x32, local copies, waits for them, and re-layouts  3.25 us
    pallas_call x2, Pallas kernels, face_flux(): pl.pallas_call(functools.partial(face_kernel, start), in_specs=[smem, sme...  3.17 us
  transfers between devices with their start and end apart: 6, of which 3 were waited for; matrix products, arithmetic and copies ran while one was open for 0% of the time, Pallas kernels for 30%

profile of v1, /device:TPU:0, one launch (start us, length us, event | category | flops | bytes accessed | tf_op | source)
XLA Modules:
  0.0 65.4 jit_solution(10994200207762419509)
XLA Ops:
  0.6 0.0 copy-start.4
  0.6 0.0 copy-start.13
  0.7 0.0 copy-start.14
  0.7 0.0 copy-start.15
  0.7 2.5 %prepare.1 = (bf16[2,256,1024]{2,1,0:T(8,128)(2,1)S(1)}, f32[4,1024]{1,0:T(4,128)S(1)}, bf16[16,16,128]{2,1,0:T(8,128)(2,1)}) custom-call(s32[1]{0:T(128)} %bitcast.core_ref, s32[1]{0:T(128)} %bitcast.1.slab_ref, f32[2,256,1024]{2,1,0:T(8,128)} %p_hbm.3, s32[2,256,1024]{2,1,0:T(8,128)} %k_hbm.3, f32[1,2048]{1,0:T(1,128)} %bitcast.13, bf16[24,2048]{1,0:T(8,128)(2,1)} %basis_hbm.2), custom_call_target="tpu_custom_call" | custom-call | tf_op jit(solution)/shard_map/prepare/pallas_call | solution.py:110
  3.2 4.9 %collective-permute-start.1 = (bf16[2,256,1024]{2,1,0:T(8,128)(2,1)S(1)}, bf16[2,256,1024]{2,1,0:T(8,128)(2,1)S(1)}, u32[]{:S(2)}, u32[]{:S(2)}) collective-permute-start(bf16[2,256,1024]{2,1,0:T(8,128)(2,1)S(1)} %get-tuple-element.22), channel_id=1, source_target_pairs={{0,2},{2,4},{4,6},{6,8},{8,10},{10,12},{12,14},{14,16},{16,18},{18... | collective-permute-start | bytes 3145736 | tf_op jit(solution)/shard_map/ppermute | solution.py:542
  8.1 0.0 copy-done.4
  8.1 0.0 copy-done.13
  8.1 0.0 copy-done.14
  8.1 0.0 copy-done.15
  8.2 0.0 copy-start.9
  8.2 8.5 %cells.1 = (f32[1,2048]{1,0:T(1,128)S(1)}, f32[2,256,1024]{2,1,0:T(8,128)S(1)}, f32[2,256,1024]{2,1,0:T(8,128)S(1)}, s32[2,256,1024]{2,1,0:T(8,128)S(1)}) custom-call(s32[1]{0:T(128)} %bitcast.core_ref, f32[2,256,1024]{2,1,0:T(8,128)} %p_hbm.3, s32[2,256,1024]{2,1,0:T(8,128)} %k_hbm.3, s32[3,2048]{1,0:T(4,128)S(1)} %copy-done.13, f32[3,2048]{1,0:T(4,128)S(1)} %copy-done.14, ...), custom_call_target="tpu_custom_call" | custom-call | flops 6442450944 | bytes 4194304 | tf_op jit(solution)/shard_map/cells/pallas_call | solution.py:213
  16.7 0.0 copy-start
  16.7 0.0 copy-start.2
  16.7 13.7 %collective-permute-done.1.halo_ref = bf16[2,256,1024]{2,1,0:T(8,128)(2,1)S(1)} collective-permute-done((bf16[2,256,1024]{2,1,0:T(8,128)(2,1)S(1)}, bf16[2,256,1024]{2,1,0:T(8,128)(2,1)S(1)}, u32[]{:S(2)}, u32[]{:S(2)}) %collective-permute-start.1) | collective-permute-done | bytes 1048608 | tf_op jit(solution)/shard_map/ppermute | solution.py:542
  30.4 0.0 copy-done.9
  30.5 1.6 %face.2.rest_0_ = bf16[128,1024]{1,0:T(8,128)(2,1)S(1)} custom-call(s32[1]{0:T(128)} %bitcast.1.slab_ref, f32[16]{0:T(128)S(1)} %copy-done.9, bf16[2,256,1024]{2,1,0:T(8,128)(2,1)S(1)} %collective-permute-done.1.halo_ref, f32[2,256,1024]{2,1,0:T(8,128)S(1)} %get-tuple-element.18.p_ref, s32[2,256,1024]{2,1,0:T(8,128)S(1)} %get-tuple-element.19.k_ref.region_ref), custom_call_target="tpu_custom_call" | custom-call | tf_op jit(solution)/shard_map/face/pallas_call | solution.py:343
  32.0 1.3 %collective-permute-start.3 = (bf16[128,1024]{1,0:T(8,128)(2,1)S(1)}, bf16[128,1024]{1,0:T(8,128)(2,1)S(1)}, u32[]{:S(2)}, u32[]{:S(2)}) collective-permute-start(bf16[128,1024]{1,0:T(8,128)(2,1)S(1)} %face.2.rest_0_), channel_id=1, source_target_pairs={{2,0},{4,2},{6,4},{8,6},{10,8},{12,10},{14,12},{16,14},{18,16},{20... | collective-permute-start | bytes 786440 | tf_op jit(solution)/shard_map/ppermute | solution.py:553
  33.3 0.0 copy-done
  33.4 0.0 copy-done.2
  33.4 1.6 %face.3.rest_1_ = bf16[128,1024]{1,0:T(8,128)(2,1)S(1)} custom-call(s32[1]{0:T(128)} %bitcast.1.slab_ref, f32[16]{0:T(128)S(1)} %copy-done.9, bf16[2,256,1024]{2,1,0:T(8,128)(2,1)S(1)} %collective-permute-done.1.halo_ref, f32[2,256,1024]{2,1,0:T(8,128)S(1)} %get-tuple-element.18.p_ref, s32[2,256,1024]{2,1,0:T(8,128)S(1)} %get-tuple-element.19.k_ref.region_ref), custom_call_target="tpu_custom_call" | custom-call | tf_op jit(solution)/shard_map/face/pallas_call | solution.py:343
  35.0 1.3 %collective-permute-start.4 = (bf16[128,1024]{1,0:T(8,128)(2,1)S(1)}, bf16[128,1024]{1,0:T(8,128)(2,1)S(1)}, u32[]{:S(2)}, u32[]{:S(2)}) collective-permute-start(bf16[128,1024]{1,0:T(8,128)(2,1)S(1)} %face.3.rest_1_), channel_id=1, source_target_pairs={{2,0},{4,2},{6,4},{8,6},{10,8},{12,10},{14,12},{16,14},{18,16},{20... | collective-permute-start | bytes 786440 | tf_op jit(solution)/shard_map/ppermute | solution.py:553
  36.3 11.9 %all-to-all-start = ((bf16[16,16,128]{2,1,0:T(8,128)(2,1)}), bf16[16,16,128]{2,1,0:T(8,128)(2,1)S(1)}, u32[]{:S(2)}, u32[]{:S(2)}) async-start(bf16[16,16,128]{2,1,0:T(8,128)(2,1)} %get-tuple-element.17), calls=%async_computation | async-start | bytes 131072 | tf_op jit(solution)/shard_map/all_to_all | solution.py:543
  48.2 0.1 collective-permute-start
  48.3 1.2 %collective-permute-done.edge_ref = f32[4,1024]{1,0:T(4,128)S(1)} collective-permute-done((f32[4,1024]{1,0:T(4,128)S(1)}, f32[4,1024]{1,0:T(4,128)S(1)}, u32[]{:S(2)}, u32[]{:S(2)}) %collective-permute-start) | collective-permute-done | bytes 16416 | tf_op jit(solution)/shard_map/ppermute | solution.py:544
  49.5 0.0 copy-start.1
  49.5 1.6 %copy-done.1 = f32[2,256,1024]{2,1,0:T(8,128)S(1)} copy-done((f32[2,256,1024]{2,1,0:T(8,128)S(1)}, f32[2,256,1024]{2,1,0:T(8,128)}, u32[]{:S(2)}) %copy-start.1) | copy-done | bytes 2097176
  51.0 0.0 copy-start.3
  51.0 1.6 %copy-done.3 = s32[2,256,1024]{2,1,0:T(8,128)S(1)} copy-done((s32[2,256,1024]{2,1,0:T(8,128)S(1)}, s32[2,256,1024]{2,1,0:T(8,128)}, u32[]{:S(2)}) %copy-start.3) | copy-done | bytes 2097176
  52.6 0.0 copy-start.10
  52.6 0.0 copy-start.11
  52.6 0.0 copy-start.12
  52.6 6.1 %stencil.1.acc_ref = f32[2,256,1024]{2,1,0:T(8,128)S(1)} custom-call(s32[1]{0:T(128)} %bitcast.core_ref, f32[16]{0:T(128)S(1)} %copy-done.9, f32[2,256,1024]{2,1,0:T(8,128)S(1)} %copy-done.1, s32[2,256,1024]{2,1,0:T(8,128)S(1)} %copy-done.3, f32[4,1024]{1,0:T(4,128)S(1)} %collective-permute-done.edge_ref, ...), custom_call_target="tpu_custom_call", output_to_operand_aliasing={{}: (5, {})} | custom-call | flops 104857600 | bytes 8388608 | tf_op jit(solution)/shard_map/stencil/pallas_call | solution.py:307
  58.7 0.0 all-to-all-done.got_ref
  58.7 0.0 copy-done.10
  58.8 0.0 copy-done.11
  58.8 0.0 copy-done.12
  58.8 0.0 copy-start.5
  58.8 0.0 copy-start.6
  58.8 0.0 copy-start.7
  58.8 0.0 copy-start.8
  58.8 3.7 %traction.1 = (f32[2,2048]{1,0:T(2,128)S(1)}, f32[2,256,1024]{2,1,0:T(8,128)}) custom-call(s32[1]{0:T(128)} %bitcast.core_ref, s32[1]{0:T(128)} %bitcast.1.slab_ref, bf16[16,16,128]{2,1,0:T(8,128)(2,1)S(1)} %all-to-all-done.got_ref, f32[1,2048]{1,0:T(1,128)S(1)} %get-tuple-element.25.sampled_ref, f32[1,2048]{1,0:T(1,128)S(1)} %bitcast.15, ...), custom_call_target="tpu_custom_call" | custom-call | tf_op jit(solution)/shard_map/traction/pallas_call | solution.py:480
  62.5 0.2 collective-permute-start.2
  62.7 1.0 %collective-permute-done.2.theirs_ref = f32[2,2048]{1,0:T(2,128)S(1)} collective-permute-done((f32[2,2048]{1,0:T(2,128)S(1)}, f32[2,2048]{1,0:T(2,128)S(1)}, u32[]{:S(2)}, u32[]{:S(2)}) %collective-permute-start.2) | collective-permute-done | bytes 16416 | tf_op jit(solution)/shard_map/ppermute | solution.py:572
  63.7 0.0 collective-permute-done.3.rest_0_
  63.7 0.0 collective-permute-done.4.rest_1_
  63.7 0.0 copy-done.5
  63.7 0.0 copy-done.6
  63.8 0.0 copy-done.7
  63.8 0.0 copy-done.8
  63.8 1.6 %finish.1 = (f32[2,256,1024]{2,1,0:T(8,128)}, f32[1,2048]{1,0:T(1,128)}, f32[1,2048]{1,0:T(1,128)}) custom-call(f32[2,256,1024]{2,1,0:T(8,128)S(1)} %stencil.1.acc_ref, f32[2,2048]{1,0:T(2,128)S(1)} %get-tuple-element.26.mine_ref, f32[2,2048]{1,0:T(2,128)S(1)} %collective-permute-done.2.theirs_ref, ...), custom_call_target="tpu_custom_call", output_to_operand_aliasing={{0}: (10, {})} | custom-call | tf_op jit(solution)/shard_map/finish/pallas_call | solution.py:381
Async XLA Ops:
  0.6 7.5 %copy-start.4 = (f32[2048]{0:T(1024)S(1)}, f32[2048]{0:T(1024)}, u32[]{:S(2)}) copy-start(f32[2048]{0:T(1024)} %param.18) | copy-start | bytes 24580
  0.6 7.5 %copy-start.13 = (s32[3,2048]{1,0:T(4,128)S(1)}, s32[3,2048]{1,0:T(4,128)}, u32[]{:S(2)}) copy-start(s32[3,2048]{1,0:T(4,128)} %corner_ref.1) | copy-start | bytes 73732
  0.7 7.5 %copy-start.14 = (f32[3,2048]{1,0:T(4,128)S(1)}, f32[3,2048]{1,0:T(4,128)}, u32[]{:S(2)}) copy-start(f32[3,2048]{1,0:T(4,128)} %fraction_ref.1) | copy-start | bytes 73732
  0.7 7.5 %copy-start.15 = (f32[2048]{0:T(1024)S(1)}, f32[2048]{0:T(1024)}, u32[]{:S(2)}) copy-start(f32[2048]{0:T(1024)} %param.23) | copy-start | bytes 24580
  3.2 27.3 %collective-permute-start.1 = (bf16[2,256,1024]{2,1,0:T(8,128)(2,1)S(1)}, bf16[2,256,1024]{2,1,0:T(8,128)(2,1)S(1)}, u32[]{:S(2)}, u32[]{:S(2)}) collective-permute-start(bf16[2,256,1024]{2,1,0:T(8,128)(2,1)S(1)} %get-tuple-element.22), channel_id=1, source_target_pairs={{0,2},{2,4},{4,6},{6,8},{8,10},{10,12},{12,14},{14,16},{16,18},{18... | collective-permute-start | bytes 3145736 | tf_op jit(solution)/shard_map/ppermute | solution.py:542
  8.2 22.3 %copy-start.9 = (f32[16]{0:T(128)S(1)}, f32[16]{0:T(128)}, u32[]{:S(2)}) copy-start(f32[16]{0:T(128)} %perm_ref.5) | copy-start | bytes 196
  16.7 16.6 %copy-start = (f32[2,256,1024]{2,1,0:T(8,128)}, f32[2,256,1024]{2,1,0:T(8,128)S(1)}, u32[]{:S(2)}) copy-start(f32[2,256,1024]{2,1,0:T(8,128)S(1)} %get-tuple-element.18.p_ref) | copy-start | bytes 6291460
  16.7 16.6 %copy-start.2 = (s32[2,256,1024]{2,1,0:T(8,128)}, s32[2,256,1024]{2,1,0:T(8,128)S(1)}, u32[]{:S(2)}) copy-start(s32[2,256,1024]{2,1,0:T(8,128)S(1)} %get-tuple-element.19.k_ref.region_ref) | copy-start | bytes 6291460
  32.0 31.7 %collective-permute-start.3 = (bf16[128,1024]{1,0:T(8,128)(2,1)S(1)}, bf16[128,1024]{1,0:T(8,128)(2,1)S(1)}, u32[]{:S(2)}, u32[]{:S(2)}) collective-permute-start(bf16[128,1024]{1,0:T(8,128)(2,1)S(1)} %face.2.rest_0_), channel_id=1, source_target_pairs={{2,0},{4,2},{6,4},{8,6},{10,8},{12,10},{14,12},{16,14},{18,16},{20... | collective-permute-start | bytes 786440 | tf_op jit(solution)/shard_map/ppermute | solution.py:553
  35.0 28.8 %collective-permute-start.4 = (bf16[128,1024]{1,0:T(8,128)(2,1)S(1)}, bf16[128,1024]{1,0:T(8,128)(2,1)S(1)}, u32[]{:S(2)}, u32[]{:S(2)}) collective-permute-start(bf16[128,1024]{1,0:T(8,128)(2,1)S(1)} %face.3.rest_1_), channel_id=1, source_target_pairs={{2,0},{4,2},{6,4},{8,6},{10,8},{12,10},{14,12},{16,14},{18,16},{20... | collective-permute-start | bytes 786440 | tf_op jit(solution)/shard_map/ppermute | solution.py:553
  36.3 22.5 %all-to-all-start = ((bf16[16,16,128]{2,1,0:T(8,128)(2,1)}), bf16[16,16,128]{2,1,0:T(8,128)(2,1)S(1)}, u32[]{:S(2)}, u32[]{:S(2)}) async-start(bf16[16,16,128]{2,1,0:T(8,128)(2,1)} %get-tuple-element.17), calls=%async_computation | async-start | bytes 131072 | tf_op jit(solution)/shard_map/all_to_all | solution.py:543
  48.2 1.2 %collective-permute-start = (f32[4,1024]{1,0:T(4,128)S(1)}, f32[4,1024]{1,0:T(4,128)S(1)}, u32[]{:S(2)}, u32[]{:S(2)}) collective-permute-start(f32[4,1024]{1,0:T(4,128)S(1)} %get-tuple-element.20), channel_id=1, source_target_pairs={{0,1},{1,0},{2,3},{3,2},{4,5},{5,4},{6,7},{7,6},{8,9},{9,8},{10,11... | collective-permute-start | bytes 49160 | tf_op jit(solution)/shard_map/ppermute | solution.py:544
  49.5 1.6 %copy-start.1 = (f32[2,256,1024]{2,1,0:T(8,128)S(1)}, f32[2,256,1024]{2,1,0:T(8,128)}, u32[]{:S(2)}) copy-start(f32[2,256,1024]{2,1,0:T(8,128)} %copy-done) | copy-start | bytes 6291460
  51.0 1.6 %copy-start.3 = (s32[2,256,1024]{2,1,0:T(8,128)S(1)}, s32[2,256,1024]{2,1,0:T(8,128)}, u32[]{:S(2)}) copy-start(s32[2,256,1024]{2,1,0:T(8,128)} %copy-done.2) | copy-start | bytes 6291460
  52.6 6.1 %copy-start.10 = (s32[1024]{0:T(1024)S(1)}, s32[1024]{0:T(1024)}, u32[]{:S(2)}) copy-start(s32[1024]{0:T(1024)} %param.29) | copy-start | bytes 12292
  52.6 6.1 %copy-start.11 = (s32[1024]{0:T(1024)S(1)}, s32[1024]{0:T(1024)}, u32[]{:S(2)}) copy-start(s32[1024]{0:T(1024)} %param.30) | copy-start | bytes 12292
  52.6 6.1 %copy-start.12 = (s32[1024]{0:T(1024)S(1)}, s32[1024]{0:T(1024)}, u32[]{:S(2)}) copy-start(s32[1024]{0:T(1024)} %param.31) | copy-start | bytes 12292
  58.8 5.0 %copy-start.5 = (f32[2048]{0:T(1024)S(1)}, f32[2048]{0:T(1024)}, u32[]{:S(2)}) copy-start(f32[2048]{0:T(1024)} %param.19) | copy-start | bytes 24580
  58.8 5.0 %copy-start.6 = (f32[2048]{0:T(1024)S(1)}, f32[2048]{0:T(1024)}, u32[]{:S(2)}) copy-start(f32[2048]{0:T(1024)} %param.20) | copy-start | bytes 24580
  58.8 5.0 %copy-start.7 = (f32[2048]{0:T(1024)S(1)}, f32[2048]{0:T(1024)}, u32[]{:S(2)}) copy-start(f32[2048]{0:T(1024)} %param.21) | copy-start | bytes 24580
  58.8 5.0 %copy-start.8 = (f32[2048]{0:T(1024)S(1)}, f32[2048]{0:T(1024)}, u32[]{:S(2)}) copy-start(f32[2048]{0:T(1024)} %param.22) | copy-start | bytes 24580
  62.5 1.2 %collective-permute-start.2 = (f32[2,2048]{1,0:T(2,128)S(1)}, f32[2,2048]{1,0:T(2,128)S(1)}, u32[]{:S(2)}, u32[]{:S(2)}) collective-permute-start(f32[2,2048]{1,0:T(2,128)S(1)} %get-tuple-element.26.mine_ref), channel_id=1, source_target_pairs={{0,1},{1,0},{2,3},{3,2},{4,5},{5,4},{6,7},{7,6},{8,9},{9,8},{10,11... | collective-permute-start | bytes 49160 | tf_op jit(solution)/shard_map/ppermute | solution.py:572
